TPU v7x, 32 devices: a whole 2x2x4 slice. The times are simulated.
32 devices in a mesh: dp: 16 (over z, y, x), tensor: 2 (over core).
Axes of the slice: x: 2, y: 2, z: 4, core: 2. Of those that a mesh axis runs over, the one named last changes fastest.
Arguments:
- layer_input: bfloat16 [16384, 768], P('dp'), may hold values from -6 to 6
- patch_features: bfloat16 [16384, 1024], P('dp', 'tensor'), may hold values from -400 to 400
- bucket_ids: int32 [64], P('dp'), may hold values from 0 to 1
- text_lengths: int32 [64], P('dp'), may hold values from 1 to 31
- upstream: bfloat16 [16384, 768], P('dp'), may hold values from -6 to 6
- query_weight: bfloat16 [768, 768], P(None, 'tensor'), may hold values from -0.21875 to 0.21875
- key_weight: bfloat16 [768, 768], P(None, 'tensor'), may hold values from -0.21875 to 0.21875
- value_weight: bfloat16 [768, 768], P(None, 'tensor'), may hold values from -0.21875 to 0.21875
- merge_weight: bfloat16 [768, 768], P('tensor'), may hold values from -1.75 to 1.75
- query_bias: float32 [768], P('tensor'), may hold values from -3 to 3
- value_bias: float32 [768], P('tensor'), may hold values from -3 to 3
- merge_bias: float32 [768], replicated, may hold values from -3 to 3
- head_gain: float32 [12], P('tensor'), may hold values from 0.25 to 1.75
- distance_table: float32 [12, 511], P('tensor'), may hold values from -4 to 4
- first_gain: float32 [768], replicated, may hold values from 0.25 to 1.75
- first_shift: float32 [768], replicated, may hold values from -3 to 3
- second_gain: float32 [768], replicated, may hold values from 0.25 to 1.75
- second_shift: float32 [768], replicated, may hold values from -3 to 3
- expand_weight: bfloat16 [768, 3072], P(None, 'tensor'), may hold values from -0.21875 to 0.21875
- expand_bias: float32 [3072], P('tensor'), may hold values from -3 to 3
- reduce_weight: bfloat16 [3072, 768], P('tensor'), may hold values from -0.15625 to 0.15625
- reduce_bias: float32 [768], replicated, may hold values from -3 to 3
- image_weight: bfloat16 [1024, 768], P('tensor'), may hold values from -0.1875 to 0.1875
- stem_gain: float32 [1024], P('tensor'), may hold values from 0.25 to 1.75
- stem_shift: float32 [1024], P('tensor'), may hold values from -3 to 3
Outputs:
- block_output: bfloat16 [16384, 768], P('dp')
- input_grad: float32 [16384, 768], P('dp')
- patch_grad: float32 [16384, 1024], P('dp', 'tensor')
- grad_query_weight: float32 [768, 768], P(None, 'tensor')
- grad_key_weight: float32 [768, 768], P(None, 'tensor')
- grad_value_weight: float32 [768, 768], P(None, 'tensor')
- grad_merge_weight: float32 [768, 768], P('tensor')
- grad_query_bias: float32 [768], P('tensor')
- grad_value_bias: float32 [768], P('tensor')
- grad_merge_bias: float32 [768], replicated
- grad_head_gain: float32 [12], P('tensor')
- grad_distance_table: float32 [12, 511], P('tensor')
- grad_first_gain: float32 [768], replicated
- grad_first_shift: float32 [768], replicated
- grad_second_gain: float32 [768], replicated
- grad_second_shift: float32 [768], replicated
- grad_expand_weight: float32 [768, 3072], P(None, 'tensor')
- grad_expand_bias: float32 [3072], P('tensor')
- grad_reduce_weight: float32 [3072, 768], P('tensor')
- grad_reduce_bias: float32 [768], replicated
- grad_image_weight: float32 [1024, 768], P('tensor')
- grad_stem_gain: float32 [1024], P('tensor')
- grad_stem_shift: float32 [1024], P('tensor')
All inputs are finite; a program needn't handle non-finite values.
Results may differ from a plain program's by a relative error of at most 0.014.
Values sent between devices are 32-bit elements; how exact they have to be, the bound alone decides.
No kernel may reach another device: no remote copies, remote signals or barrier semaphores. Data moves between devices by JAX's collectives and lax.ppermute only.
A program may use at most 128 MiB of HBM per device.

v0:
```python
from functools import partial
import jax
import jax.numpy as jnp
from jax import lax
from jax.sharding import PartitionSpec as P

HEAD_DIM = 64
PATCH_SMALL = 64
PATCH_LARGE = 225
EPSILON = 1e-05
NEGATIVE = -1e30


def layer_norm(values, gain, shift):
    centered = values - jnp.mean(values, axis=-1, keepdims=True)
    scaled = centered * lax.rsqrt(jnp.mean(centered * centered, axis=-1, keepdims=True) + EPSILON)
    return scaled * gain + shift


def distance_bias(table, length):
    count_heads = table.shape[0]
    padded = jnp.pad(table, ((0, 0), (0, 1)))
    tiled = jnp.broadcast_to(padded[:, None, :], (count_heads, length, 2 * length)).reshape(
        count_heads, 2 * length * length
    )
    window = tiled[:, length - 1 : length - 1 + length * (2 * length - 1)].reshape(
        count_heads, length, 2 * length - 1
    )
    return window[:, :, :length]


def scores_of(query_low, key_low, bias, key_valid, scale):
    scores = (
        jnp.einsum("bqhd,bkhd->bhqk", query_low, key_low, preferred_element_type=jnp.float32)
        * scale
        + bias[None]
    )
    return jnp.where(key_valid[:, None, None, :], scores, NEGATIVE)


def project_back(grad_low, weight):
    return jnp.einsum("tf,df->td", grad_low, weight, preferred_element_type=jnp.float32)


def weight_grad(inputs_low, grad_low):
    return jnp.einsum("tc,td->cd", inputs_low, grad_low, preferred_element_type=jnp.float32)


def swap_core(values):
    count = lax.axis_size("tensor")
    pairs = [(core, core ^ 1) for core in range(count)]
    return values + lax.ppermute(values, "tensor", pairs)


def exchange(values, bit):
    count = lax.axis_size("dp")
    pairs = [(rank, rank ^ 1 << bit) for rank in range(count)]
    return lax.ppermute(values, "dp", pairs)


def sum_by_doubling(values):
    for bit in range(lax.axis_size("dp").bit_length() - 1):
        values = values + exchange(values, bit)
    return values


def sum_by_halving(values, order):
    rank = lax.axis_index("dp")
    for bit in order:
        half = values.shape[0] // 2
        side = rank >> bit & 1
        sent = lax.dynamic_slice_in_dim(values, (1 - side) * half, half, 0)
        kept = lax.dynamic_slice_in_dim(values, side * half, half, 0)
        values = kept + exchange(sent, bit)
    for bit in reversed(order):
        side = rank >> bit & 1
        other = exchange(values, bit)
        values = jnp.where(
            side == 1, jnp.concatenate([other, values]), jnp.concatenate([values, other])
        )
    return values


def orders():
    bits = tuple(range(lax.axis_size("dp").bit_length() - 1))
    return (bits, (bits[1], bits[0]) + bits[2:])


def pack(arrays):
    flat = jnp.concatenate([entry.reshape(-1) for entry in arrays])
    short = -flat.shape[0] % 1024
    return jnp.pad(flat, (0, short)).reshape(-1, 128)


def unpack(packed, arrays):
    flat, at, parts = (packed.reshape(-1), 0, [])
    for entry in arrays:
        parts.append(flat[at : at + entry.size].reshape(entry.shape))
        at += entry.size
    return parts


def local(
    layer_input,
    patch_features,
    bucket_ids,
    text_lengths,
    upstream,
    query_weight,
    key_weight,
    value_weight,
    merge_weight,
    query_bias,
    value_bias,
    merge_bias,
    head_gain,
    distance_table,
    first_gain,
    first_shift,
    second_gain,
    second_shift,
    expand_weight,
    expand_bias,
    reduce_weight,
    reduce_bias,
    image_weight,
    stem_gain,
    stem_shift,
):
    items = bucket_ids.shape[0]
    rows = layer_input.shape[0]
    length = rows // items
    heads = head_gain.shape[0]
    width = query_weight.shape[1]
    scale = HEAD_DIM ** (-0.5)
    patches = PATCH_SMALL + (PATCH_LARGE - PATCH_SMALL) * bucket_ids
    slots = jnp.arange(length, dtype=jnp.int32)
    patch_mask = (slots[None, :] < patches[:, None]).astype(jnp.float32).reshape(rows)
    key_valid = slots[None, :] < (patches + text_lengths)[:, None]
    valid_rows = key_valid.astype(jnp.float32).reshape(rows)
    features = patch_features.astype(jnp.float32)
    masked = features * patch_mask[:, None]
    feature_sum, square_sum, count = sum_by_doubling(
        jnp.stack(
            [
                jnp.sum(masked, axis=0),
                jnp.sum(masked * features, axis=0),
                jnp.full((features.shape[1],), jnp.sum(patch_mask)),
            ]
        )
    )
    stem_mean = feature_sum / count
    stem_inverse = lax.rsqrt(square_sum / count - stem_mean * stem_mean + EPSILON)
    stem_hat = (features - stem_mean) * stem_inverse
    stem_low = (stem_hat * stem_gain + stem_shift).astype(jnp.bfloat16)
    embedded = swap_core(jnp.dot(stem_low, image_weight, preferred_element_type=jnp.float32))
    hidden = layer_input.astype(jnp.float32) + patch_mask[:, None] * embedded
    first_normed, first_back = jax.vjp(layer_norm, hidden, first_gain, first_shift)
    first_low = first_normed.astype(jnp.bfloat16)
    split_shape = (items, length, heads, HEAD_DIM)
    query_low = (
        (jnp.dot(first_low, query_weight, preferred_element_type=jnp.float32) + query_bias)
        .astype(jnp.bfloat16)
        .reshape(split_shape)
    )
    key_low = (
        jnp.dot(first_low, key_weight, preferred_element_type=jnp.float32)
        .astype(jnp.bfloat16)
        .reshape(split_shape)
    )
    value_low = (
        (jnp.dot(first_low, value_weight, preferred_element_type=jnp.float32) + value_bias)
        .astype(jnp.bfloat16)
        .reshape(split_shape)
    )
    bias, bias_back = jax.vjp(lambda table: distance_bias(table, length), distance_table)
    scores = scores_of(query_low, key_low, bias, key_valid, scale)
    peak = jnp.max(scores, axis=-1, keepdims=True)
    log_total = peak + jnp.log(jnp.sum(jnp.exp(scores - peak), axis=-1, keepdims=True))
    probs_low = jnp.exp(scores - log_total).astype(jnp.bfloat16)
    mixed = jnp.einsum("bhqk,bkhd->bqhd", probs_low, value_low, preferred_element_type=jnp.float32)
    scaled_low = (mixed * head_gain[None, None, :, None]).astype(jnp.bfloat16).reshape(rows, width)
    branch = swap_core(jnp.dot(scaled_low, merge_weight, preferred_element_type=jnp.float32))
    middle = hidden + branch + merge_bias
    second_normed, second_back = jax.vjp(layer_norm, middle, second_gain, second_shift)
    second_low = second_normed.astype(jnp.bfloat16)
    expanded = jnp.dot(second_low, expand_weight, preferred_element_type=jnp.float32) + expand_bias
    active, gelu_back = jax.vjp(partial(jax.nn.gelu, approximate=False), expanded)
    active_low = active.astype(jnp.bfloat16)
    reduced = swap_core(jnp.dot(active_low, reduce_weight, preferred_element_type=jnp.float32))
    block_output = (middle + reduced + reduce_bias).astype(jnp.bfloat16)
    grad_result = upstream.astype(jnp.float32) * valid_rows[:, None]
    grad_reduce_bias = jnp.sum(grad_result, axis=0)
    grad_reduced_low = grad_result.astype(jnp.bfloat16)
    grad_reduce_weight = weight_grad(active_low, grad_reduced_low)
    (grad_expanded,) = gelu_back(project_back(grad_reduced_low, reduce_weight))
    grad_expanded_low = grad_expanded.astype(jnp.bfloat16)
    grad_expand_bias = jnp.sum(grad_expanded_low.astype(jnp.float32), axis=0)
    grad_expand_weight = weight_grad(second_low, grad_expanded_low)
    grad_second = swap_core(project_back(grad_expanded_low, expand_weight))
    grad_middle_part, grad_second_gain, grad_second_shift = second_back(grad_second)
    grad_middle = grad_result + grad_middle_part
    grad_merge_bias = jnp.sum(grad_middle, axis=0)
    grad_branch_low = grad_middle.astype(jnp.bfloat16)
    grad_merge_weight = weight_grad(scaled_low, grad_branch_low)
    grad_scaled = project_back(grad_branch_low, merge_weight).reshape(split_shape)
    grad_head_gain = jnp.sum(grad_scaled * mixed, axis=(0, 1, 3))
    grad_mixed_low = (grad_scaled * head_gain[None, None, :, None]).astype(jnp.bfloat16)
    again = scores_of(query_low, key_low, bias, key_valid, scale)
    probs = jnp.exp(again - log_total)
    probs_again = probs.astype(jnp.bfloat16)
    grad_value_low = jnp.einsum(
        "bhqk,bqhd->bkhd", probs_again, grad_mixed_low, preferred_element_type=jnp.float32
    ).astype(jnp.bfloat16)
    grad_probs = jnp.einsum(
        "bqhd,bkhd->bhqk", grad_mixed_low, value_low, preferred_element_type=jnp.float32
    )
    grad_scores = probs * (grad_probs - jnp.sum(probs * grad_probs, axis=-1, keepdims=True))
    grad_scores_low = grad_scores.astype(jnp.bfloat16)
    (grad_distance_table,) = bias_back(jnp.sum(grad_scores_low.astype(jnp.float32), axis=0))
    grad_query_low = (
        (
            jnp.einsum(
                "bhqk,bkhd->bqhd", grad_scores_low, key_low, preferred_element_type=jnp.float32
            )
            * scale
        )
        .astype(jnp.bfloat16)
        .reshape(rows, width)
    )
    grad_key_low = (
        (
            jnp.einsum(
                "bhqk,bqhd->bkhd", grad_scores_low, query_low, preferred_element_type=jnp.float32
            )
            * scale
        )
        .astype(jnp.bfloat16)
        .reshape(rows, width)
    )
    grad_value_low = grad_value_low.reshape(rows, width)
    grad_query_bias = jnp.sum(grad_query_low.astype(jnp.float32), axis=0)
    grad_value_bias = jnp.sum(grad_value_low.astype(jnp.float32), axis=0)
    grad_heads_low = jnp.concatenate([grad_query_low, grad_key_low, grad_value_low], axis=1)
    grad_heads_weight = weight_grad(first_low, grad_heads_low)
    grad_first_part = (
        project_back(grad_query_low, query_weight)
        + project_back(grad_key_low, key_weight)
        + project_back(grad_value_low, value_weight)
    )
    grad_first = swap_core(grad_first_part)
    grad_hidden_part, grad_first_gain, grad_first_shift = first_back(grad_first)
    input_grad = grad_middle + grad_hidden_part
    grad_embedded_low = (input_grad * patch_mask[:, None]).astype(jnp.bfloat16)
    grad_image_weight = weight_grad(stem_low, grad_embedded_low)
    grad_stem = project_back(grad_embedded_low, image_weight)
    shift_local = jnp.sum(grad_stem, axis=0)
    gain_local = jnp.sum(grad_stem * stem_hat, axis=0)
    first_order, second_order = orders()
    grad_reduce_weight = lax.psum(grad_reduce_weight, "dp")
    grad_expand_weight = sum_by_halving(grad_expand_weight, second_order)
    merge_rows = grad_merge_weight.shape[0]
    row_weights = sum_by_halving(
        jnp.concatenate([grad_merge_weight, grad_image_weight]), second_order
    )
    grad_merge_weight, grad_image_weight = (row_weights[:merge_rows], row_weights[merge_rows:])
    grad_heads_weight = sum_by_halving(grad_heads_weight, first_order)
    grad_query_weight = grad_heads_weight[:, :width]
    grad_key_weight = grad_heads_weight[:, width : 2 * width]
    grad_value_weight = grad_heads_weight[:, 2 * width :]
    small = (
        grad_query_bias,
        grad_value_bias,
        grad_merge_bias,
        grad_head_gain,
        grad_distance_table,
        grad_first_gain,
        grad_first_shift,
        grad_second_gain,
        grad_second_shift,
        grad_expand_bias,
        grad_reduce_bias,
        gain_local,
        shift_local,
    )
    (
        grad_query_bias,
        grad_value_bias,
        grad_merge_bias,
        grad_head_gain,
        grad_distance_table,
        grad_first_gain,
        grad_first_shift,
        grad_second_gain,
        grad_second_shift,
        grad_expand_bias,
        grad_reduce_bias,
        grad_stem_gain,
        grad_stem_shift,
    ) = unpack(sum_by_doubling(pack(small)), small)
    patch_grad = (
        patch_mask[:, None]
        * stem_inverse
        * stem_gain
        * (grad_stem - grad_stem_shift / count - stem_hat * grad_stem_gain / count)
    )
    return (
        block_output,
        input_grad,
        patch_grad,
        grad_query_weight,
        grad_key_weight,
        grad_value_weight,
        grad_merge_weight,
        grad_query_bias,
        grad_value_bias,
        grad_merge_bias,
        grad_head_gain,
        grad_distance_table,
        grad_first_gain,
        grad_first_shift,
        grad_second_gain,
        grad_second_shift,
        grad_expand_weight,
        grad_expand_bias,
        grad_reduce_weight,
        grad_reduce_bias,
        grad_image_weight,
        grad_stem_gain,
        grad_stem_shift,
    )


def solution(mesh):
    in_specs = (
        P("dp", None),
        P("dp", "tensor"),
        P("dp"),
        P("dp"),
        P("dp", None),
        P(None, "tensor"),
        P(None, "tensor"),
        P(None, "tensor"),
        P("tensor", None),
        P("tensor"),
        P("tensor"),
        P(),
        P("tensor"),
        P("tensor", None),
        P(),
        P(),
        P(),
        P(),
        P(None, "tensor"),
        P("tensor"),
        P("tensor", None),
        P(),
        P("tensor", None),
        P("tensor"),
        P("tensor"),
    )
    out_specs = (
        P("dp", None),
        P("dp", None),
        P("dp", "tensor"),
        P(None, "tensor"),
        P(None, "tensor"),
        P(None, "tensor"),
        P("tensor", None),
        P("tensor"),
        P("tensor"),
        P(),
        P("tensor"),
        P("tensor", None),
        P(),
        P(),
        P(),
        P(),
        P(None, "tensor"),
        P("tensor"),
        P("tensor", None),
        P(),
        P("tensor", None),
        P("tensor"),
        P("tensor"),
    )
    return jax.shard_map(local, mesh=mesh, in_specs=in_specs, out_specs=out_specs, check_vma=False)
```

profile of v0, /device:TPU:0, one launch (start us, length us, event | category | flops | bytes accessed | tf_op | source)
XLA Modules:
  0.0 607.6 jit_solution(3583659250479429453)
XLA Ops:
  11.3 3.0 collective-permute-start
  23.4 3.0 collective-permute-start.3
  28.8 4.2 fusion.58
  33.1 3.1 copy.166
  38.5 3.2 slice.125
  41.6 6.4 %reshape.255 = f32[6,256,511]{2,1,0:T(8,128)} reshape(f32[6,130816]{1,0:T(8,128)} %slice.125) | data formatting | bytes 6279168 | tf_op jit(solution)/shard_map/jvp()/reshape | solution.py:26
  50.8 3.0 copy.172
  53.9 4.2 fusion.77
  65.0 3.4 add_convert_fusion.4
  73.6 3.4 add_convert_fusion.5
  81.9 3.3 fusion.79
  96.9 3.0 collective-permute-done.5
  100.0 4.2 fusion.76
  105.1 19.0 %multiply_convert_fusion.1 = (bf16[1024,1536]{1,0:T(8,128)(2,1)S(1)}, f32[1024,1536]{1,0:T(8,128)}, f32[1024,1536]{1,0:T(8,128)}) fusion(f32[1536]{0:T(1024)S(1)} %copy-done.66, bf16[768,1536]{1,0:T(8,128)(2,1)S(1)} %copy-done, f32[1024,768]{0,1:T(8,128)S(1)} %get-tuple-element.159, f32[768]{0:T(1024)S(1)} %copy-done.67, f32[768]{0:T(1024)S(1)} %copy-done.52, ...), kind=kOutput, calls=%fused_computation.7 | convolution fusion | flops 2523660288 | bytes 21254144 | tf_op jit(solution)/shard_map/dot_general | solution.py:187
  124.1 9.3 %convert_reduce_fusion = (f32[1536]{0:T(1024)S(1)}, bf16[1024,1536]{1,0:T(8,128)(2,1)S(1)}) fusion(f32[1024,1536]{1,0:T(8,128)} %get-tuple-element.157, bf16[1536,768]{1,0:T(8,128)(2,1)S(1)} %copy-done.65, bf16[1024,768]{0,1:T(8,128)(2,1)S(1)} %copy-done.23, f32[1024]{0:T(1024)S(1)} %bitcast.158, f32[1024,1536]{1,0:T(8,128)} %get-tuple-element.190, ...), kind=kOutput, calls=%fused_computation.2 | convolution fusion | flops 2445015552 | bytes 19677184 | tf_op jit(solution)/shard_map/tf,df->td/dot_general | solution.py:42
  139.9 4.4 fusion.82
  144.3 4.3 fusion.81
  149.1 42.9 %collective-permute-done.29 = f32[384,1536]{1,0:T(8,128)} collective-permute-done((f32[384,1536]{1,0:T(8,128)}, f32[384,1536]{1,0:T(8,128)}, u32[]{:S(2)}, u32[]{:S(2)}) %collective-permute-start.29) | collective-permute-done | bytes 2359328 | tf_op jit(solution)/shard_map/ppermute | solution.py:58
  197.6 4.0 fusion.71
  203.0 5.3 fusion.74
  214.1 5.0 convert_reduce_fusion.2
  219.1 7.2 %multiply_reduce_fusion = (f32[4,6,256]{2,1,0:T(8,128)S(1)}, f32[4,6,256,256]{2,3,1,0:T(8,128)}) fusion(f32[4,6,256,256]{2,3,1,0:T(8,128)} %copy-done.2, f32[4,6,256]{2,1,0:T(8,128)S(1)} %log_add_fusion, bf16[4,256,6,64]{1,0,3,2:T(4,128)(2,1)S(1)} %copy-done.17, f32[4,256,6,64]{1,0,3,2:T(4,128)S(1)} %reshape.257, f32[6]{0:T(128)S(1)} %copy-done.60), kind=kOutput, calls=%fused_computation.5 | convolution fusion | flops 206825472 | bytes 14991384 | tf_op jit(solution)/shard_map/bqhd,bkhd->bhqk/dot_general | solution.py:215
  226.3 6.0 convert_reduce_fusion.1
  237.9 3.0 copy.209
  244.7 6.6 %reshape.261 = f32[6,130816]{1,0:T(8,128)} reshape(f32[6,256,511]{2,1,0:T(8,128)} %pad.20.clone) | data formatting | bytes 6279168 | tf_op jit(solution)/shard_map/transpose(jvp())/reshape | solution.py:26
  251.3 3.7 pad.21
  255.0 4.0 fusion.10
  270.4 11.1 %collective-permute-done.31 = f32[96,1536]{1,0:T(8,128)S(1)} collective-permute-done((f32[96,1536]{1,0:T(8,128)S(1)}, f32[96,1536]{1,0:T(8,128)S(1)}, u32[]{:S(2)}, u32[]{:S(2)}) %collective-permute-start.31) | collective-permute-done | bytes 589856 | tf_op jit(solution)/shard_map/ppermute | solution.py:58
  284.2 18.0 %collective-permute-done.13 = f32[384,1152]{1,0:T(8,128)S(1)} collective-permute-done((f32[384,1152]{1,0:T(8,128)S(1)}, f32[384,1152]{1,0:T(8,128)S(1)}, u32[]{:S(2)}, u32[]{:S(2)}) %collective-permute-start.13) | collective-permute-done | bytes 1769504 | tf_op jit(solution)/shard_map/ppermute | solution.py:58
  307.6 10.8 %collective-permute-done.33 = f32[48,1536]{1,0:T(8,128)S(1)} collective-permute-done((f32[48,1536]{1,0:T(8,128)S(1)}, f32[48,1536]{1,0:T(8,128)S(1)}, u32[]{:S(2)}, u32[]{:S(2)}) %collective-permute-start.33) | collective-permute-done | bytes 294944 | tf_op jit(solution)/shard_map/ppermute | solution.py:58
  336.3 7.1 %collective-permute-done.15 = f32[96,1152]{1,0:T(8,128)} collective-permute-done((f32[96,1152]{1,0:T(8,128)}, f32[96,1152]{1,0:T(8,128)}, u32[]{:S(2)}, u32[]{:S(2)}) %collective-permute-start.15) | collective-permute-done | bytes 442400 | tf_op jit(solution)/shard_map/ppermute | solution.py:58
  345.2 3.3 collective-permute-start.16
  348.5 13.7 %collective-permute-done.10 = f32[88,128]{1,0:T(8,128)S(1)} collective-permute-done((f32[88,128]{1,0:T(8,128)S(1)}, f32[88,128]{1,0:T(8,128)S(1)}, u32[]{:S(2)}, u32[]{:S(2)}) %collective-permute-start.10) | collective-permute-done | bytes 45088 | tf_op jit(solution)/shard_map/ppermute | solution.py:58
  372.8 3.3 collective-permute-done.17
  377.2 5.8 collective-permute-done.22
  385.3 4.3 fusion.29
  392.6 3.7 copy.198
  403.3 11.8 %collective-permute-done.35 = f32[192,1536]{1,0:T(8,128)} collective-permute-done((f32[192,1536]{1,0:T(8,128)}, f32[192,1536]{1,0:T(8,128)}, u32[]{:S(2)}, u32[]{:S(2)}) %collective-permute-start.35) | collective-permute-done | bytes 1179680 | tf_op jit(solution)/shard_map/ppermute | solution.py:58
  415.2 3.0 maximum_select_fusion.3
  423.3 13.6 %collective-permute-done.25 = f32[56,768]{1,0:T(8,128)S(1)} collective-permute-done((f32[56,768]{1,0:T(8,128)S(1)}, f32[56,768]{1,0:T(8,128)S(1)}, u32[]{:S(2)}, u32[]{:S(2)}) %collective-permute-start.25) | collective-permute-done | bytes 172064 | tf_op jit(solution)/shard_map/ppermute | solution.py:58
  440.0 13.1 %collective-permute-done.26 = f32[112,768]{1,0:T(8,128)S(1)} collective-permute-done((f32[112,768]{1,0:T(8,128)S(1)}, f32[112,768]{1,0:T(8,128)S(1)}, u32[]{:S(2)}, u32[]{:S(2)}) %collective-permute-start.26) | collective-permute-done | bytes 344096 | tf_op jit(solution)/shard_map/ppermute | solution.py:58
  458.2 35.2 %collective-permute-done.27 = f32[224,768]{1,0:T(8,128)S(1)} collective-permute-done((f32[224,768]{1,0:T(8,128)S(1)}, f32[224,768]{1,0:T(8,128)S(1)}, u32[]{:S(2)}, u32[]{:S(2)}) %collective-permute-start.27) | collective-permute-done | bytes 688160 | tf_op jit(solution)/shard_map/ppermute | solution.py:58
  498.2 5.3 maximum_select_fusion
  503.5 3.6 maximum_select_fusion.1
  509.0 12.9 %collective-permute-done.28 = f32[448,768]{1,0:T(8,128)} collective-permute-done((f32[448,768]{1,0:T(8,128)}, f32[448,768]{1,0:T(8,128)}, u32[]{:S(2)}, u32[]{:S(2)}) %collective-permute-start.28) | collective-permute-done | bytes 1376288 | tf_op jit(solution)/shard_map/ppermute | solution.py:58
  522.0 3.3 maximum_select_fusion.2
  527.6 68.0 %all-reduce.6.cloned.1.call-done = f32[1536,768]{1,0:T(8,128)} async-done(((f32[1536,768]{1,0:T(8,128)}), f32[1536,768]{1,0:T(8,128)}) %all-reduce.6.cloned.1.call-update) | async-done | bytes 4718608 | tf_op jit(solution)/shard_map/psum | solution.py:260
  595.6 5.0 copy.250
  (331 shorter events, 164.2 us)
Async XLA Ops:
  7.2 97.5 %copy-start = (bf16[768,1536]{1,0:T(8,128)(2,1)S(1)}, bf16[768,1536]{1,0:T(8,128)(2,1)}, u32[]{:S(2)}) copy-start(bf16[768,1536]{1,0:T(8,128)(2,1)} %param.43) | copy-start | bytes 7077892
  7.2 588.4 %all-reduce.6.cloned.1.call-start = ((), (), s32[]{:S(2)}) async-start(), calls=%async_computation | async-start | bytes 9437184 | tf_op jit(solution)/shard_map/psum | solution.py:260
  8.8 45.1 %copy-start.44 = (f32[1,2,4,128]{3,1,2,0:T(2,128)}, f32[1,2,4,128]{3,1,2,0:T(2,128)S(1)}, u32[]{:S(2)}) copy-start(f32[1,2,4,128]{3,1,2,0:T(2,128)S(1)} %copy.210) | copy-start | bytes 12292
  11.3 4.6 collective-permute-start
  16.0 3.7 collective-permute-start.1
  19.7 3.7 collective-permute-start.2
  23.4 4.7 collective-permute-start.3
  33.0 20.9 %collective-permute-start.4 = (f32[1024,768]{0,1:T(8,128)}, f32[1024,768]{0,1:T(8,128)}, u32[]{:S(2)}, u32[]{:S(2)}) collective-permute-start(f32[1024,768]{0,1:T(8,128)} %fusion.58), channel_id=1, source_target_pairs={{0,1},{1,0},{2,3},{3,2},{4,5},{5,4},{6,7},{7,6},{8,9},{9,8},{10,11... | collective-permute-start | bytes 9437192 | tf_op jit(solution)/shard_map/ppermute | solution.py:52
  93.9 6.1 %collective-permute-start.5 = (f32[1024,768]{0,1:T(8,128)}, f32[1024,768]{0,1:T(8,128)}, u32[]{:S(2)}, u32[]{:S(2)}) collective-permute-start(f32[1024,768]{0,1:T(8,128)} %fusion.80), channel_id=1, source_target_pairs={{0,1},{1,0},{2,3},{3,2},{4,5},{5,4},{6,7},{7,6},{8,9},{9,8},{10,11... | collective-permute-start | bytes 9437192 | tf_op jit(solution)/shard_map/ppermute | solution.py:52
  104.2 29.2 %copy-start.5 = (f32[1024,768]{0,1:T(8,128)}, f32[1024,768]{0,1:T(8,128)S(1)}, u32[]{:S(2)}) copy-start(f32[1024,768]{0,1:T(8,128)S(1)} %get-tuple-element.159) | copy-start | bytes 9437188
  137.9 54.0 %collective-permute-start.29 = (f32[384,1536]{1,0:T(8,128)}, f32[384,1536]{1,0:T(8,128)}, u32[]{:S(2)}, u32[]{:S(2)}) collective-permute-start(f32[384,1536]{1,0:T(8,128)} %constant_dynamic-slice_fusion.3), channel_id=1, source_target_pairs={{0,4},{2,6},{4,0},{6,2},{8,12},{10,14},{12,8},{14,10},{16,20},{18,... | collective-permute-start | bytes 7077896 | tf_op jit(solution)/shard_map/ppermute | solution.py:58
  144.2 53.4 %collective-permute-start.7 = (f32[1024,768]{0,1:T(8,128)}, f32[1024,768]{0,1:T(8,128)}, u32[]{:S(2)}, u32[]{:S(2)}) collective-permute-start(f32[1024,768]{0,1:T(8,128)} %fusion.82), channel_id=1, source_target_pairs={{0,1},{1,0},{2,3},{3,2},{4,5},{5,4},{6,7},{7,6},{8,9},{9,8},{10,11... | collective-permute-start | bytes 9437192 | tf_op jit(solution)/shard_map/ppermute | solution.py:52
  148.7 54.2 %collective-permute-start.6 = (f32[1024,768]{0,1:T(8,128)}, f32[1024,768]{0,1:T(8,128)}, u32[]{:S(2)}, u32[]{:S(2)}) collective-permute-start(f32[1024,768]{0,1:T(8,128)} %fusion.81), channel_id=1, source_target_pairs={{0,1},{1,0},{2,3},{3,2},{4,5},{5,4},{6,7},{7,6},{8,9},{9,8},{10,11... | collective-permute-start | bytes 9437192 | tf_op jit(solution)/shard_map/ppermute | solution.py:52
  149.1 48.5 %copy-start.6 = (f32[1024,768]{0,1:T(8,128)S(1)}, f32[1024,768]{0,1:T(8,128)}, u32[]{:S(2)}) copy-start(f32[1024,768]{0,1:T(8,128)} %copy-done.5) | copy-start | bytes 9437188
  195.9 68.9 %collective-permute-start.30 = (f32[192,1536]{1,0:T(8,128)}, f32[192,1536]{1,0:T(8,128)}, u32[]{:S(2)}, u32[]{:S(2)}) collective-permute-start(f32[192,1536]{1,0:T(8,128)} %constant_dynamic-slice_fusion.2), channel_id=1, source_target_pairs={{0,2},{2,0},{4,6},{6,4},{8,10},{10,8},{12,14},{14,12},{16,18},{18,... | collective-permute-start | bytes 3538952 | tf_op jit(solution)/shard_map/ppermute | solution.py:58
  262.4 39.8 %collective-permute-start.13 = (f32[384,1152]{1,0:T(8,128)S(1)}, f32[384,1152]{1,0:T(8,128)S(1)}, u32[]{:S(2)}, u32[]{:S(2)}) collective-permute-start(f32[384,1152]{1,0:T(8,128)S(1)} %constant_dynamic-slice_fusion.10), channel_id=1, source_target_pairs={{0,2},{2,0},{4,6},{6,4},{8,10},{10,8},{12,14},{14,12},{16,18},{18,... | collective-permute-start | bytes 5308424 | tf_op jit(solution)/shard_map/ppermute | solution.py:58
  267.0 14.4 %collective-permute-start.31 = (f32[96,1536]{1,0:T(8,128)S(1)}, f32[96,1536]{1,0:T(8,128)S(1)}, u32[]{:S(2)}, u32[]{:S(2)}) collective-permute-start(f32[96,1536]{1,0:T(8,128)S(1)} %constant_dynamic-slice_fusion.1), channel_id=1, source_target_pairs={{0,8},{2,10},{4,12},{6,14},{8,0},{10,2},{12,4},{14,6},{16,24},{18,... | collective-permute-start | bytes 1769480 | tf_op jit(solution)/shard_map/ppermute | solution.py:58
  269.9 32.4 %copy-start.29 = (f32[768,1152]{1,0:T(8,128)S(1)}, f32[768,1152]{1,0:T(8,128)}, u32[]{:S(2)}) copy-start(f32[768,1152]{1,0:T(8,128)} %fusion.10) | copy-start | bytes 10616836
  269.9 55.2 %collective-permute-start.8 = (f32[1024,768]{0,1:T(8,128)S(1)}, f32[1024,768]{0,1:T(8,128)S(1)}, u32[]{:S(2)}, u32[]{:S(2)}) collective-permute-start(f32[1024,768]{0,1:T(8,128)S(1)} %add_add_fusion.3), channel_id=1, source_target_pairs={{0,1},{1,0},{2,3},{3,2},{4,5},{5,4},{6,7},{7,6},{8,9},{9,8},{10,11... | collective-permute-start | bytes 9437192 | tf_op jit(solution)/shard_map/ppermute | solution.py:52
  281.6 25.2 %copy-start.8 = (f32[1024,768]{0,1:T(8,128)S(1)}, f32[1024,768]{0,1:T(8,128)}, u32[]{:S(2)}) copy-start(f32[1024,768]{0,1:T(8,128)} %copy-done.7) | copy-start | bytes 9437188
  281.6 25.1 %copy-start.11 = (bf16[48,8,4,256]{3,1,2,0:T(8,128)(2,1)S(1)}, bf16[48,8,4,256]{3,1,2,0:T(8,128)(2,1)}, u32[]{:S(2)}) copy-start(bf16[48,8,4,256]{3,1,2,0:T(8,128)(2,1)} %copy-done.10) | copy-start | bytes 2359300
  281.6 22.5 %collective-permute-start.32 = (f32[48,1536]{1,0:T(8,128)S(1)}, f32[48,1536]{1,0:T(8,128)S(1)}, u32[]{:S(2)}, u32[]{:S(2)}) collective-permute-start(f32[48,1536]{1,0:T(8,128)S(1)} %constant_dynamic-slice_fusion), channel_id=1, source_target_pairs={{0,16},{2,18},{4,20},{6,22},{8,24},{10,26},{12,28},{14,30},{16,0},... | collective-permute-start | bytes 884744 | tf_op jit(solution)/shard_map/ppermute | solution.py:58
  302.5 20.0 %collective-permute-start.14 = (f32[192,1152]{1,0:T(8,128)S(1)}, f32[192,1152]{1,0:T(8,128)S(1)}, u32[]{:S(2)}, u32[]{:S(2)}) collective-permute-start(f32[192,1152]{1,0:T(8,128)S(1)} %constant_dynamic-slice_fusion.9), channel_id=1, source_target_pairs={{0,4},{2,6},{4,0},{6,2},{8,12},{10,14},{12,8},{14,10},{16,20},{18,... | collective-permute-start | bytes 2654216 | tf_op jit(solution)/shard_map/ppermute | solution.py:58
  304.2 14.3 %collective-permute-start.33 = (f32[48,1536]{1,0:T(8,128)S(1)}, f32[48,1536]{1,0:T(8,128)S(1)}, u32[]{:S(2)}, u32[]{:S(2)}) collective-permute-start(f32[48,1536]{1,0:T(8,128)S(1)} %dynamic-slice_add_fusion.8), channel_id=1, source_target_pairs={{0,16},{2,18},{4,20},{6,22},{8,24},{10,26},{12,28},{14,30},{16,0},... | collective-permute-start | bytes 884744 | tf_op jit(solution)/shard_map/ppermute | solution.py:58
  319.3 49.0 %collective-permute-start.34 = (f32[96,1536]{1,0:T(8,128)}, f32[96,1536]{1,0:T(8,128)}, u32[]{:S(2)}, u32[]{:S(2)}) collective-permute-start(f32[96,1536]{1,0:T(8,128)} %maximum_select_fusion.9), channel_id=1, source_target_pairs={{0,8},{2,10},{4,12},{6,14},{8,0},{10,2},{12,4},{14,6},{16,24},{18,... | collective-permute-start | bytes 1769480 | tf_op jit(solution)/shard_map/ppermute | solution.py:58
  323.5 19.9 %collective-permute-start.15 = (f32[96,1152]{1,0:T(8,128)}, f32[96,1152]{1,0:T(8,128)}, u32[]{:S(2)}, u32[]{:S(2)}) collective-permute-start(f32[96,1152]{1,0:T(8,128)} %constant_dynamic-slice_fusion.8), channel_id=1, source_target_pairs={{0,8},{2,10},{4,12},{6,14},{8,0},{10,2},{12,4},{14,6},{16,24},{18,... | collective-permute-start | bytes 1327112 | tf_op jit(solution)/shard_map/ppermute | solution.py:58
  331.7 31.1 %collective-permute-start.21 = (f32[448,768]{1,0:T(8,128)}, f32[448,768]{1,0:T(8,128)}, u32[]{:S(2)}, u32[]{:S(2)}) collective-permute-start(f32[448,768]{1,0:T(8,128)} %fusion.35), channel_id=1, source_target_pairs={{0,4},{2,6},{4,0},{6,2},{8,12},{10,14},{12,8},{14,10},{16,20},{18,... | collective-permute-start | bytes 4128776 | tf_op jit(solution)/shard_map/ppermute | solution.py:58
  335.7 27.1 %copy-start.22 = (f32[512,768]{1,0:T(8,128)S(1)}, f32[512,768]{1,0:T(8,128)}, u32[]{:S(2)}) copy-start(f32[512,768]{1,0:T(8,128)} %copy-done.21) | copy-start | bytes 4718596
  335.7 8.9 %collective-permute-start.9 = (f32[88,128]{1,0:T(8,128)S(1)}, f32[88,128]{1,0:T(8,128)S(1)}, u32[]{:S(2)}, u32[]{:S(2)}) collective-permute-start(f32[88,128]{1,0:T(8,128)S(1)} %pad_bitcast_fusion), channel_id=1, source_target_pairs={{0,2},{2,0},{4,6},{6,4},{8,10},{10,8},{12,14},{14,12},{16,18},{18,... | collective-permute-start | bytes 135176 | tf_op jit(solution)/shard_map/ppermute | solution.py:58
  344.6 17.5 %collective-permute-start.10 = (f32[88,128]{1,0:T(8,128)S(1)}, f32[88,128]{1,0:T(8,128)S(1)}, u32[]{:S(2)}, u32[]{:S(2)}) collective-permute-start(f32[88,128]{1,0:T(8,128)S(1)} %fusion.65), channel_id=1, source_target_pairs={{0,4},{2,6},{4,0},{6,2},{8,12},{10,14},{12,8},{14,10},{16,20},{18,... | collective-permute-start | bytes 135176 | tf_op jit(solution)/shard_map/ppermute | solution.py:58
  345.2 20.3 %collective-permute-start.16 = (f32[48,1152]{1,0:T(8,128)S(1)}, f32[48,1152]{1,0:T(8,128)S(1)}, u32[]{:S(2)}, u32[]{:S(2)}) collective-permute-start(f32[48,1152]{1,0:T(8,128)S(1)} %constant_dynamic-slice_fusion.7), channel_id=1, source_target_pairs={{0,16},{2,18},{4,20},{6,22},{8,24},{10,26},{12,28},{14,30},{16,0},... | collective-permute-start | bytes 663560 | tf_op jit(solution)/shard_map/ppermute | solution.py:58
  362.2 10.4 %collective-permute-start.11 = (f32[88,128]{1,0:T(8,128)S(1)}, f32[88,128]{1,0:T(8,128)S(1)}, u32[]{:S(2)}, u32[]{:S(2)}) collective-permute-start(f32[88,128]{1,0:T(8,128)S(1)} %fusion.114), channel_id=1, source_target_pairs={{0,8},{2,10},{4,12},{6,14},{8,0},{10,2},{12,4},{14,6},{16,24},{18,... | collective-permute-start | bytes 135176 | tf_op jit(solution)/shard_map/ppermute | solution.py:58
  364.6 18.4 %collective-permute-start.22 = (f32[224,768]{1,0:T(8,128)S(1)}, f32[224,768]{1,0:T(8,128)S(1)}, u32[]{:S(2)}, u32[]{:S(2)}) collective-permute-start(f32[224,768]{1,0:T(8,128)S(1)} %constant_dynamic-slice_fusion.6), channel_id=1, source_target_pairs={{0,2},{2,0},{4,6},{6,4},{8,10},{10,8},{12,14},{14,12},{16,18},{18,... | collective-permute-start | bytes 2064392 | tf_op jit(solution)/shard_map/ppermute | solution.py:58
  365.6 10.5 %collective-permute-start.17 = (f32[48,1152]{1,0:T(8,128)S(1)}, f32[48,1152]{1,0:T(8,128)S(1)}, u32[]{:S(2)}, u32[]{:S(2)}) collective-permute-start(f32[48,1152]{1,0:T(8,128)S(1)} %dynamic-slice_add_fusion.9), channel_id=1, source_target_pairs={{0,16},{2,18},{4,20},{6,22},{8,24},{10,26},{12,28},{14,30},{16,0},... | collective-permute-start | bytes 663560 | tf_op jit(solution)/shard_map/ppermute | solution.py:58
  371.1 44.0 %collective-permute-start.35 = (f32[192,1536]{1,0:T(8,128)}, f32[192,1536]{1,0:T(8,128)}, u32[]{:S(2)}, u32[]{:S(2)}) collective-permute-start(f32[192,1536]{1,0:T(8,128)} %maximum_select_fusion.6), channel_id=1, source_target_pairs={{0,2},{2,0},{4,6},{6,4},{8,10},{10,8},{12,14},{14,12},{16,18},{18,... | collective-permute-start | bytes 3538952 | tf_op jit(solution)/shard_map/ppermute | solution.py:58
  372.6 23.7 %collective-permute-start.12 = (f32[88,128]{1,0:T(8,128)S(1)}, f32[88,128]{1,0:T(8,128)S(1)}, u32[]{:S(2)}, u32[]{:S(2)}) collective-permute-start(f32[88,128]{1,0:T(8,128)S(1)} %add.330), channel_id=1, source_target_pairs={{0,16},{2,18},{4,20},{6,22},{8,24},{10,26},{12,28},{14,30},{16,0},... | collective-permute-start | bytes 135176 | tf_op jit(solution)/shard_map/ppermute | solution.py:58
  376.9 19.4 %collective-permute-start.18 = (f32[96,1152]{1,0:T(8,128)}, f32[96,1152]{1,0:T(8,128)}, u32[]{:S(2)}, u32[]{:S(2)}) collective-permute-start(f32[96,1152]{1,0:T(8,128)} %maximum_select_fusion.10), channel_id=1, source_target_pairs={{0,8},{2,10},{4,12},{6,14},{8,0},{10,2},{12,4},{14,6},{16,24},{18,... | collective-permute-start | bytes 1327112 | tf_op jit(solution)/shard_map/ppermute | solution.py:58
  383.8 15.9 %collective-permute-start.23 = (f32[112,768]{1,0:T(8,128)}, f32[112,768]{1,0:T(8,128)}, u32[]{:S(2)}, u32[]{:S(2)}) collective-permute-start(f32[112,768]{1,0:T(8,128)} %constant_dynamic-slice_fusion.5), channel_id=1, source_target_pairs={{0,8},{2,10},{4,12},{6,14},{8,0},{10,2},{12,4},{14,6},{16,24},{18,... | collective-permute-start | bytes 1032200 | tf_op jit(solution)/shard_map/ppermute | solution.py:58
  398.0 39.6 %collective-permute-start.19 = (f32[192,1152]{1,0:T(8,128)S(1)}, f32[192,1152]{1,0:T(8,128)S(1)}, u32[]{:S(2)}, u32[]{:S(2)}) collective-permute-start(f32[192,1152]{1,0:T(8,128)S(1)} %maximum_select_fusion.7), channel_id=1, source_target_pairs={{0,4},{2,6},{4,0},{6,2},{8,12},{10,14},{12,8},{14,10},{16,20},{18,... | collective-permute-start | bytes 2654216 | tf_op jit(solution)/shard_map/ppermute | solution.py:58
  400.8 21.2 %collective-permute-start.24 = (f32[56,768]{1,0:T(8,128)S(1)}, f32[56,768]{1,0:T(8,128)S(1)}, u32[]{:S(2)}, u32[]{:S(2)}) collective-permute-start(f32[56,768]{1,0:T(8,128)S(1)} %constant_dynamic-slice_fusion.4), channel_id=1, source_target_pairs={{0,16},{2,18},{4,20},{6,22},{8,24},{10,26},{12,28},{14,30},{16,0},... | collective-permute-start | bytes 516104 | tf_op jit(solution)/shard_map/ppermute | solution.py:58
  418.1 38.0 %copy-start.15 = (f32[1024,512]{1,0:T(8,128)S(1)}, f32[1024,512]{1,0:T(8,128)}, u32[]{:S(2)}) copy-start(f32[1024,512]{1,0:T(8,128)} %get-tuple-element.199) | copy-start | bytes 6291460
  418.1 80.1 %collective-permute-start.36 = (f32[384,1536]{1,0:T(8,128)S(1)}, f32[384,1536]{1,0:T(8,128)}, u32[]{:S(2)}, u32[]{:S(2)}) collective-permute-start(f32[384,1536]{1,0:T(8,128)S(1)} %maximum_select_fusion.3), channel_id=1, source_target_pairs={{0,4},{2,6},{4,0},{6,2},{8,12},{10,14},{12,8},{14,10},{16,20},{18,... | collective-permute-start | bytes 7077896 | tf_op jit(solution)/shard_map/ppermute | solution.py:58
  422.0 14.9 %collective-permute-start.25 = (f32[56,768]{1,0:T(8,128)S(1)}, f32[56,768]{1,0:T(8,128)S(1)}, u32[]{:S(2)}, u32[]{:S(2)}) collective-permute-start(f32[56,768]{1,0:T(8,128)S(1)} %dynamic-slice_add_fusion.10), channel_id=1, source_target_pairs={{0,16},{2,18},{4,20},{6,22},{8,24},{10,26},{12,28},{14,30},{16,0},... | collective-permute-start | bytes 516104 | tf_op jit(solution)/shard_map/ppermute | solution.py:58
  437.0 16.1 %collective-permute-start.26 = (f32[112,768]{1,0:T(8,128)S(1)}, f32[112,768]{1,0:T(8,128)S(1)}, u32[]{:S(2)}, u32[]{:S(2)}) collective-permute-start(f32[112,768]{1,0:T(8,128)S(1)} %maximum_select_fusion.11), channel_id=1, source_target_pairs={{0,8},{2,10},{4,12},{6,14},{8,0},{10,2},{12,4},{14,6},{16,24},{18,... | collective-permute-start | bytes 1032200 | tf_op jit(solution)/shard_map/ppermute | solution.py:58
  437.6 20.6 %copy-start.59 = (f32[512]{0:T(512)}, f32[512]{0:T(512)S(1)}, u32[]{:S(2)}) copy-start(f32[512]{0:T(512)S(1)} %get-tuple-element.221) | copy-start | bytes 6148
  439.0 64.5 %collective-permute-start.20 = (f32[384,1152]{1,0:T(8,128)}, f32[384,1152]{1,0:T(8,128)}, u32[]{:S(2)}, u32[]{:S(2)}) collective-permute-start(f32[384,1152]{1,0:T(8,128)} %maximum_select_fusion.4), channel_id=1, source_target_pairs={{0,2},{2,0},{4,6},{6,4},{8,10},{10,8},{12,14},{14,12},{16,18},{18,... | collective-permute-start | bytes 5308424 | tf_op jit(solution)/shard_map/ppermute | solution.py:58
  453.1 40.3 %collective-permute-start.27 = (f32[224,768]{1,0:T(8,128)S(1)}, f32[224,768]{1,0:T(8,128)S(1)}, u32[]{:S(2)}, u32[]{:S(2)}) collective-permute-start(f32[224,768]{1,0:T(8,128)S(1)} %maximum_select_fusion.8), channel_id=1, source_target_pairs={{0,2},{2,0},{4,6},{6,4},{8,10},{10,8},{12,14},{14,12},{16,18},{18,... | collective-permute-start | bytes 2064392 | tf_op jit(solution)/shard_map/ppermute | solution.py:58
  494.6 27.4 %collective-permute-start.28 = (f32[448,768]{1,0:T(8,128)}, f32[448,768]{1,0:T(8,128)}, u32[]{:S(2)}, u32[]{:S(2)}) collective-permute-start(f32[448,768]{1,0:T(8,128)} %maximum_select_fusion.5), channel_id=1, source_target_pairs={{0,4},{2,6},{4,0},{6,2},{8,12},{10,14},{12,8},{14,10},{16,20},{18,... | collective-permute-start | bytes 4128776 | tf_op jit(solution)/shard_map/ppermute | solution.py:58
  (65 other events, 324.3 us)
Sparse Core Ops, SparseCore 0:
  389.8 205.7 all-reduce.5
where the time goes:
time: 611 us; the launch traced here: 608 us
  waiting for transfers between devices  282 us (46%)
  local copies, waits for them, and re-layouts  93.4 us (15%)
  matrix products  92.9 us (15%)
  other arithmetic  73.4 us (12%)
  starting transfers between devices  50.9 us (8%)
  between operations  15.3 us (3%)
    ppermute x32, waiting for transfers between devices, exchange(): return lax.ppermute(values, 'dp', pairs)  211 us
    psum x1, waiting for transfers between devices, local(): grad_reduce_weight = lax.psum(grad_reduce_weight, 'dp')  68 us
    ppermute x32, starting transfers between devices, exchange(): return lax.ppermute(values, 'dp', pairs)  49.7 us
    unnamed x164, local copies, waits for them, and re-layouts  31.4 us
    select_n x12, other arithmetic, sum_by_halving(): jnp.where(side == 1, jnp.concatenate([other, values]), jnp.concatenate([v...  24 us
    dot_general x7, matrix products, project_back(): jnp.einsum('tf,df->td', grad_low, weight, preferred_element_type=jnp.floa...  21 us
    dot_general x1, matrix products, local(): jnp.dot(second_low, expand_weight, preferred_element_type=jnp.float32)  19 us
    dot_general x5, matrix products, weight_grad(): jnp.einsum('tc,td->cd', inputs_low, grad_low, preferred_element_type=jnp....  13.3 us
  transfers between devices with their start and end apart: 38, of which 21 were waited for; matrix products, arithmetic and copies ran while one was open for 27% of the time, Pallas kernels for 0%

commit v1 on v0

--- a/solution.py
+++ b/solution.py
@@ -257,7 +257,11 @@
     shift_local = jnp.sum(grad_stem, axis=0)
     gain_local = jnp.sum(grad_stem * stem_hat, axis=0)
     first_order, second_order = orders()
-    grad_reduce_weight = lax.psum(grad_reduce_weight, "dp")
+    grad_reduce_weight = grad_reduce_weight
+    for hop in (1, 2, 4, 8):
+        grad_reduce_weight = grad_reduce_weight + lax.ppermute(
+            grad_reduce_weight, "dp", [(dev, dev ^ hop) for dev in range(16)]
+        )
     grad_expand_weight = sum_by_halving(grad_expand_weight, second_order)
     merge_rows = grad_merge_weight.shape[0]
     row_weights = sum_by_halving(

time: 611 us -> 914 us (1.50)
  waiting for transfers between devices: 282 us -> 554 us
  other arithmetic: 73.4 us -> 106 us
  between operations: 15.3 us -> 2.12 us
    ppermute x32, waiting for transfers between devices: 211 us -> 551 us  [exchange(): return lax.ppermute(values, 'dp', pairs)]
    psum x1 -> x0, waiting for transfers between devices: 68 us -> none  [local(): grad_reduce_weight = lax.psum(grad_reduce_weight, 'dp')]
    add x0 -> x4, other arithmetic: none -> 26.4 us  [local(): grad_reduce_weight + lax.ppermute(grad_reduce_weight, 'dp', [(dev, dev ^...]
    unnamed x164 -> x173, local copies, waits for them, and re-layouts: 31.4 us -> 24.7 us
  transfers between devices with their start and end apart: 38 -> 41, of which waited for: 21 -> 21; matrix products, arithmetic and copies ran while one was open for 27% -> 21% of each run, Pallas kernels for 0% -> 0%
where the time goes in v1:
time: 914 us; the launch traced here: 903 us
  waiting for transfers between devices  554 us (61%)
  other arithmetic  106 us (12%)
  matrix products  94.9 us (10%)
  local copies, waits for them, and re-layouts  89.8 us (10%)
  starting transfers between devices  56.1 us (6%)
    ppermute x32, waiting for transfers between devices, exchange(): return lax.ppermute(values, 'dp', pairs)  551 us
    ppermute x32, starting transfers between devices, exchange(): return lax.ppermute(values, 'dp', pairs)  49.3 us
    add x4, other arithmetic, local(): grad_reduce_weight + lax.ppermute(grad_reduce_weight, 'dp', [(dev, dev ^...  26.4 us
    unnamed x173, local copies, waits for them, and re-layouts  24.7 us
    dot_general x7, matrix products, project_back(): jnp.einsum('tf,df->td', grad_low, weight, preferred_element_type=jnp.floa...  23.2 us
    select_n x12, other arithmetic, sum_by_halving(): jnp.where(side == 1, jnp.concatenate([other, values]), jnp.concatenate([v...  20.9 us
    dot_general x1, matrix products, local(): jnp.dot(second_low, expand_weight, preferred_element_type=jnp.float32)  19.3 us
  transfers between devices with their start and end apart: 41, of which 21 were waited for; matrix products, arithmetic and copies ran while one was open for 21% of the time, Pallas kernels for 0%

profile of v1, /device:TPU:0, one launch (start us, length us, event | category | flops | bytes accessed | tf_op | source)
XLA Modules:
  0.0 903.5 jit_solution(12686774441578552079)
XLA Ops:
  22.2 4.2 fusion.58
  31.4 3.2 slice.125
  34.5 6.4 reshape.255
  46.8 4.2 fusion.77
  57.9 3.4 add_convert_fusion.4
  66.5 3.4 add_convert_fusion.5
  74.9 3.3 fusion.79
  89.9 3.0 collective-permute-done.5
  93.0 4.2 fusion.76
  98.1 19.3 %multiply_convert_fusion.1 = (bf16[1024,1536]{1,0:T(8,128)(2,1)S(1)}, f32[1024,1536]{1,0:T(8,128)}, f32[1024,1536]{1,0:T(8,128)}) fusion(f32[1536]{0:T(1024)S(1)} %copy-done.72, bf16[768,1536]{1,0:T(8,128)(2,1)S(1)} %copy-done, f32[1024,768]{0,1:T(8,128)S(1)} %get-tuple-element.159, f32[768]{0:T(1024)S(1)} %copy-done.73, f32[768]{0:T(1024)S(1)} %copy-done.51, ...), kind=kOutput, calls=%fused_computation.7 | convolution fusion | flops 2523660288 | bytes 21254144 | tf_op jit(solution)/shard_map/dot_general | solution.py:187
  117.4 9.7 %convert_reduce_fusion = (f32[1536]{0:T(1024)}, bf16[1024,1536]{1,0:T(8,128)(2,1)S(1)}) fusion(f32[1024,1536]{1,0:T(8,128)} %get-tuple-element.157, bf16[1536,768]{1,0:T(8,128)(2,1)S(1)} %copy-done.71, bf16[1024,768]{0,1:T(8,128)(2,1)S(1)} %copy-done.23, f32[1024]{0:T(1024)S(1)} %bitcast.158, f32[1024,1536]{1,0:T(8,128)} %get-tuple-element.190, ...), kind=kOutput, calls=%fused_computation.2 | convolution fusion | flops 2445015552 | bytes 19677184 | tf_op jit(solution)/shard_map/tf,df->td/dot_general | solution.py:42
  133.5 4.4 fusion.82
  138.0 4.4 fusion.81
  142.8 6.9 fusion.29
  151.1 34.4 %collective-permute-done.29 = f32[384,1536]{1,0:T(8,128)} collective-permute-done((f32[384,1536]{1,0:T(8,128)}, f32[384,1536]{1,0:T(8,128)}, u32[]{:S(2)}, u32[]{:S(2)}) %collective-permute-start.29) | collective-permute-done | bytes 2359328 | tf_op jit(solution)/shard_map/ppermute | solution.py:58
  190.6 4.6 fusion.71
  197.1 5.9 fusion.74
  209.0 7.3 multiply_reduce_fusion
  216.3 7.9 convert_reduce_fusion.1
  234.1 45.0 %collective-permute-done.30 = f32[192,1536]{1,0:T(8,128)} collective-permute-done((f32[192,1536]{1,0:T(8,128)}, f32[192,1536]{1,0:T(8,128)}, u32[]{:S(2)}, u32[]{:S(2)}) %collective-permute-start.30) | collective-permute-done | bytes 1179680 | tf_op jit(solution)/shard_map/ppermute | solution.py:58
  285.9 9.1 %collective-permute-done.31 = f32[96,1536]{1,0:T(8,128)S(1)} collective-permute-done((f32[96,1536]{1,0:T(8,128)S(1)}, f32[96,1536]{1,0:T(8,128)S(1)}, u32[]{:S(2)}, u32[]{:S(2)}) %collective-permute-start.31) | collective-permute-done | bytes 589856 | tf_op jit(solution)/shard_map/ppermute | solution.py:58
  299.0 6.6 add.374
  306.1 3.8 collective-permute-done.32
  315.7 3.5 pad.20.clone
  319.1 6.6 reshape.261
  325.7 3.5 pad.21
  329.3 4.1 collective-permute-start.34
  349.9 76.9 %collective-permute-done.14 = f32[192,1152]{1,0:T(8,128)} collective-permute-done((f32[192,1152]{1,0:T(8,128)}, f32[192,1152]{1,0:T(8,128)}, u32[]{:S(2)}, u32[]{:S(2)}) %collective-permute-start.14) | collective-permute-done | bytes 884768 | tf_op jit(solution)/shard_map/ppermute | solution.py:58
  429.9 4.0 fusion.72
  433.9 6.6 add.375
  456.5 20.0 %collective-permute-done.21 = f32[448,768]{1,0:T(8,128)} collective-permute-done((f32[448,768]{1,0:T(8,128)}, f32[448,768]{1,0:T(8,128)}, u32[]{:S(2)}, u32[]{:S(2)}) %collective-permute-start.21) | collective-permute-done | bytes 1376288 | tf_op jit(solution)/shard_map/ppermute | solution.py:58
  479.8 64.8 %collective-permute-done.16 = f32[48,1152]{1,0:T(8,128)S(1)} collective-permute-done((f32[48,1152]{1,0:T(8,128)S(1)}, f32[48,1152]{1,0:T(8,128)S(1)}, u32[]{:S(2)}, u32[]{:S(2)}) %collective-permute-start.16) | collective-permute-done | bytes 221216 | tf_op jit(solution)/shard_map/ppermute | solution.py:58
  544.7 3.5 collective-permute-start.17
  548.3 7.1 collective-permute-done.17
  561.5 3.8 copy.198
  565.3 8.1 collective-permute-done.12
  573.3 6.6 add.376
  579.9 3.4 collective-permute-start.40
  591.0 200.8 %collective-permute-done.24 = f32[56,768]{1,0:T(8,128)S(1)} collective-permute-done((f32[56,768]{1,0:T(8,128)S(1)}, f32[56,768]{1,0:T(8,128)S(1)}, u32[]{:S(2)}, u32[]{:S(2)}) %collective-permute-start.24) | collective-permute-done | bytes 172064 | tf_op jit(solution)/shard_map/ppermute | solution.py:58
  792.5 5.7 collective-permute-done.25
  798.2 4.3 collective-permute-start.26
  805.9 4.2 collective-permute-done.26
  814.5 44.5 %collective-permute-done.27 = f32[224,768]{1,0:T(8,128)S(1)} collective-permute-done((f32[224,768]{1,0:T(8,128)S(1)}, f32[224,768]{1,0:T(8,128)S(1)}, u32[]{:S(2)}, u32[]{:S(2)}) %collective-permute-start.27) | collective-permute-done | bytes 688160 | tf_op jit(solution)/shard_map/ppermute | solution.py:58
  863.1 5.3 maximum_select_fusion
  868.4 3.5 maximum_select_fusion.1
  873.7 17.1 %collective-permute-done.28 = f32[448,768]{1,0:T(8,128)} collective-permute-done((f32[448,768]{1,0:T(8,128)}, f32[448,768]{1,0:T(8,128)}, u32[]{:S(2)}, u32[]{:S(2)}) %collective-permute-start.28) | collective-permute-done | bytes 1376288 | tf_op jit(solution)/shard_map/ppermute | solution.py:58
  890.8 3.2 maximum_select_fusion.2
  896.4 6.7 add.377
  (349 shorter events, 179.1 us)
Async XLA Ops:
  0.7 97.0 %copy-start = (bf16[768,1536]{1,0:T(8,128)(2,1)S(1)}, bf16[768,1536]{1,0:T(8,128)(2,1)}, u32[]{:S(2)}) copy-start(bf16[768,1536]{1,0:T(8,128)(2,1)} %param.43) | copy-start | bytes 7077892
  4.7 4.6 collective-permute-start
  9.4 3.7 collective-permute-start.1
  13.1 3.7 collective-permute-start.2
  16.9 4.7 collective-permute-start.3
  26.4 20.4 %collective-permute-start.4 = (f32[1024,768]{0,1:T(8,128)}, f32[1024,768]{0,1:T(8,128)}, u32[]{:S(2)}, u32[]{:S(2)}) collective-permute-start(f32[1024,768]{0,1:T(8,128)} %fusion.58), channel_id=1, source_target_pairs={{0,1},{1,0},{2,3},{3,2},{4,5},{5,4},{6,7},{7,6},{8,9},{9,8},{10,11... | collective-permute-start | bytes 9437192 | tf_op jit(solution)/shard_map/ppermute | solution.py:52
  86.9 6.1 collective-permute-start.5
  131.6 54.0 %collective-permute-start.29 = (f32[384,1536]{1,0:T(8,128)}, f32[384,1536]{1,0:T(8,128)}, u32[]{:S(2)}, u32[]{:S(2)}) collective-permute-start(f32[384,1536]{1,0:T(8,128)} %constant_dynamic-slice_fusion.3), channel_id=1, source_target_pairs={{0,4},{2,6},{4,0},{6,2},{8,12},{10,14},{12,8},{14,10},{16,20},{18,... | collective-permute-start | bytes 7077896 | tf_op jit(solution)/shard_map/ppermute | solution.py:58
  137.9 52.7 %collective-permute-start.7 = (f32[1024,768]{0,1:T(8,128)}, f32[1024,768]{0,1:T(8,128)}, u32[]{:S(2)}, u32[]{:S(2)}) collective-permute-start(f32[1024,768]{0,1:T(8,128)} %fusion.82), channel_id=1, source_target_pairs={{0,1},{1,0},{2,3},{3,2},{4,5},{5,4},{6,7},{7,6},{8,9},{9,8},{10,11... | collective-permute-start | bytes 9437192 | tf_op jit(solution)/shard_map/ppermute | solution.py:52
  142.3 54.8 %collective-permute-start.6 = (f32[1024,768]{0,1:T(8,128)}, f32[1024,768]{0,1:T(8,128)}, u32[]{:S(2)}, u32[]{:S(2)}) collective-permute-start(f32[1024,768]{0,1:T(8,128)} %fusion.81), channel_id=1, source_target_pairs={{0,1},{1,0},{2,3},{3,2},{4,5},{5,4},{6,7},{7,6},{8,9},{9,8},{10,11... | collective-permute-start | bytes 9437192 | tf_op jit(solution)/shard_map/ppermute | solution.py:52
  149.7 149.3 %collective-permute-start.37 = (f32[1536,768]{1,0:T(8,128)}, f32[1536,768]{1,0:T(8,128)}, u32[]{:S(2)}, u32[]{:S(2)}) collective-permute-start(f32[1536,768]{1,0:T(8,128)} %fusion.29), channel_id=1, source_target_pairs={{0,2},{2,0},{4,6},{6,4},{8,10},{10,8},{12,14},{14,12},{16,18},{18,... | collective-permute-start | bytes 14155784 | tf_op jit(solution)/shard_map/ppermute | solution.py:262
  188.8 90.2 %collective-permute-start.30 = (f32[192,1536]{1,0:T(8,128)}, f32[192,1536]{1,0:T(8,128)}, u32[]{:S(2)}, u32[]{:S(2)}) collective-permute-start(f32[192,1536]{1,0:T(8,128)} %constant_dynamic-slice_fusion.2), channel_id=1, source_target_pairs={{0,2},{2,0},{4,6},{6,4},{8,10},{10,8},{12,14},{14,12},{16,18},{18,... | collective-permute-start | bytes 3538952 | tf_op jit(solution)/shard_map/ppermute | solution.py:58
  280.6 14.5 %collective-permute-start.31 = (f32[96,1536]{1,0:T(8,128)S(1)}, f32[96,1536]{1,0:T(8,128)S(1)}, u32[]{:S(2)}, u32[]{:S(2)}) collective-permute-start(f32[96,1536]{1,0:T(8,128)S(1)} %constant_dynamic-slice_fusion.1), channel_id=1, source_target_pairs={{0,8},{2,10},{4,12},{6,14},{8,0},{10,2},{12,4},{14,6},{16,24},{18,... | collective-permute-start | bytes 1769480 | tf_op jit(solution)/shard_map/ppermute | solution.py:58
  283.5 49.9 %collective-permute-start.13 = (f32[384,1152]{1,0:T(8,128)}, f32[384,1152]{1,0:T(8,128)}, u32[]{:S(2)}, u32[]{:S(2)}) collective-permute-start(f32[384,1152]{1,0:T(8,128)} %constant_dynamic-slice_fusion.10), channel_id=1, source_target_pairs={{0,2},{2,0},{4,6},{6,4},{8,10},{10,8},{12,14},{14,12},{16,18},{18,... | collective-permute-start | bytes 5308424 | tf_op jit(solution)/shard_map/ppermute | solution.py:58
  295.2 14.7 %collective-permute-start.32 = (f32[48,1536]{1,0:T(8,128)S(1)}, f32[48,1536]{1,0:T(8,128)S(1)}, u32[]{:S(2)}, u32[]{:S(2)}) collective-permute-start(f32[48,1536]{1,0:T(8,128)S(1)} %constant_dynamic-slice_fusion), channel_id=1, source_target_pairs={{0,16},{2,18},{4,20},{6,22},{8,24},{10,26},{12,28},{14,30},{16,0},... | collective-permute-start | bytes 884744 | tf_op jit(solution)/shard_map/ppermute | solution.py:58
  305.6 128.3 %collective-permute-start.38 = (f32[1536,768]{1,0:T(8,128)}, f32[1536,768]{1,0:T(8,128)}, u32[]{:S(2)}, u32[]{:S(2)}) collective-permute-start(f32[1536,768]{1,0:T(8,128)} %add.374), channel_id=1, source_target_pairs={{0,4},{2,6},{4,0},{6,2},{8,12},{10,14},{12,8},{14,10},{16,20},{18,... | collective-permute-start | bytes 14155784 | tf_op jit(solution)/shard_map/ppermute | solution.py:262
  309.9 19.3 %collective-permute-start.33 = (f32[48,1536]{1,0:T(8,128)S(1)}, f32[48,1536]{1,0:T(8,128)S(1)}, u32[]{:S(2)}, u32[]{:S(2)}) collective-permute-start(f32[48,1536]{1,0:T(8,128)S(1)} %dynamic-slice_add_fusion.8), channel_id=1, source_target_pairs={{0,16},{2,18},{4,20},{6,22},{8,24},{10,26},{12,28},{14,30},{16,0},... | collective-permute-start | bytes 884744 | tf_op jit(solution)/shard_map/ppermute | solution.py:58
  312.7 117.2 %collective-permute-start.8 = (f32[1024,768]{0,1:T(8,128)}, f32[1024,768]{0,1:T(8,128)}, u32[]{:S(2)}, u32[]{:S(2)}) collective-permute-start(f32[1024,768]{0,1:T(8,128)} %add_add_fusion.3), channel_id=1, source_target_pairs={{0,1},{1,0},{2,3},{3,2},{4,5},{5,4},{6,7},{7,6},{8,9},{9,8},{10,11... | collective-permute-start | bytes 9437192 | tf_op jit(solution)/shard_map/ppermute | solution.py:52
  329.3 18.1 %collective-permute-start.34 = (f32[96,1536]{1,0:T(8,128)S(1)}, f32[96,1536]{1,0:T(8,128)S(1)}, u32[]{:S(2)}, u32[]{:S(2)}) collective-permute-start(f32[96,1536]{1,0:T(8,128)S(1)} %maximum_select_fusion.9), channel_id=1, source_target_pairs={{0,8},{2,10},{4,12},{6,14},{8,0},{10,2},{12,4},{14,6},{16,24},{18,... | collective-permute-start | bytes 1769480 | tf_op jit(solution)/shard_map/ppermute | solution.py:58
  336.0 90.8 %collective-permute-start.14 = (f32[192,1152]{1,0:T(8,128)}, f32[192,1152]{1,0:T(8,128)}, u32[]{:S(2)}, u32[]{:S(2)}) collective-permute-start(f32[192,1152]{1,0:T(8,128)} %constant_dynamic-slice_fusion.9), channel_id=1, source_target_pairs={{0,4},{2,6},{4,0},{6,2},{8,12},{10,14},{12,8},{14,10},{16,20},{18,... | collective-permute-start | bytes 2654216 | tf_op jit(solution)/shard_map/ppermute | solution.py:58
  343.3 83.5 %copy-start.20 = (f32[384,1152]{1,0:T(8,128)S(1)}, f32[384,1152]{1,0:T(8,128)}, u32[]{:S(2)}) copy-start(f32[384,1152]{1,0:T(8,128)} %copy-done.19) | copy-start | bytes 5308420
  346.2 83.7 %copy-start.4 = (f32[1024,768]{0,1:T(8,128)S(1)}, f32[1024,768]{0,1:T(8,128)}, u32[]{:S(2)}) copy-start(f32[1024,768]{0,1:T(8,128)} %copy-done.3) | copy-start | bytes 9437188
  346.2 83.7 %copy-start.41 = (f32[1024]{0:T(1024)S(1)}, f32[1024]{0:T(1024)}, u32[]{:S(2)}) copy-start(f32[1024]{0:T(1024)} %copy-done.40) | copy-start | bytes 12292
  346.2 83.7 %copy-start.45 = (f32[768]{0:T(1024)S(1)}, f32[768]{0:T(1024)}, u32[]{:S(2)}) copy-start(f32[768]{0:T(1024)} %param.39) | copy-start | bytes 9220
  348.4 238.0 %collective-permute-start.35 = (f32[192,1536]{1,0:T(8,128)}, f32[192,1536]{1,0:T(8,128)}, u32[]{:S(2)}, u32[]{:S(2)}) collective-permute-start(f32[192,1536]{1,0:T(8,128)} %maximum_select_fusion.6), channel_id=1, source_target_pairs={{0,2},{2,0},{4,6},{6,4},{8,10},{10,8},{12,14},{14,12},{16,18},{18,... | collective-permute-start | bytes 3538952 | tf_op jit(solution)/shard_map/ppermute | solution.py:58
  428.1 19.2 %collective-permute-start.15 = (f32[96,1152]{1,0:T(8,128)S(1)}, f32[96,1152]{1,0:T(8,128)S(1)}, u32[]{:S(2)}, u32[]{:S(2)}) collective-permute-start(f32[96,1152]{1,0:T(8,128)S(1)} %constant_dynamic-slice_fusion.8), channel_id=1, source_target_pairs={{0,8},{2,10},{4,12},{6,14},{8,0},{10,2},{12,4},{14,6},{16,24},{18,... | collective-permute-start | bytes 1327112 | tf_op jit(solution)/shard_map/ppermute | solution.py:58
  440.4 132.9 %collective-permute-start.39 = (f32[1536,768]{1,0:T(8,128)}, f32[1536,768]{1,0:T(8,128)}, u32[]{:S(2)}, u32[]{:S(2)}) collective-permute-start(f32[1536,768]{1,0:T(8,128)} %add.375), channel_id=1, source_target_pairs={{0,8},{2,10},{4,12},{6,14},{8,0},{10,2},{12,4},{14,6},{16,24},{18,... | collective-permute-start | bytes 14155784 | tf_op jit(solution)/shard_map/ppermute | solution.py:262
  446.8 29.7 %collective-permute-start.21 = (f32[448,768]{1,0:T(8,128)}, f32[448,768]{1,0:T(8,128)}, u32[]{:S(2)}, u32[]{:S(2)}) collective-permute-start(f32[448,768]{1,0:T(8,128)} %fusion.35), channel_id=1, source_target_pairs={{0,4},{2,6},{4,0},{6,2},{8,12},{10,14},{12,8},{14,10},{16,20},{18,... | collective-permute-start | bytes 4128776 | tf_op jit(solution)/shard_map/ppermute | solution.py:58
  450.8 4.1 collective-permute-start.9
  452.4 92.3 %collective-permute-start.16 = (f32[48,1152]{1,0:T(8,128)S(1)}, f32[48,1152]{1,0:T(8,128)S(1)}, u32[]{:S(2)}, u32[]{:S(2)}) collective-permute-start(f32[48,1152]{1,0:T(8,128)S(1)} %constant_dynamic-slice_fusion.7), channel_id=1, source_target_pairs={{0,16},{2,18},{4,20},{6,22},{8,24},{10,26},{12,28},{14,30},{16,0},... | collective-permute-start | bytes 663560 | tf_op jit(solution)/shard_map/ppermute | solution.py:58
  454.9 93.3 %collective-permute-start.10 = (f32[88,128]{1,0:T(8,128)S(1)}, f32[88,128]{1,0:T(8,128)S(1)}, u32[]{:S(2)}, u32[]{:S(2)}) collective-permute-start(f32[88,128]{1,0:T(8,128)S(1)} %fusion.65), channel_id=1, source_target_pairs={{0,4},{2,6},{4,0},{6,2},{8,12},{10,14},{12,8},{14,10},{16,20},{18,... | collective-permute-start | bytes 135176 | tf_op jit(solution)/shard_map/ppermute | solution.py:58
  478.2 81.7 %copy-start.22 = (bf16[1024,768]{0,1:T(8,128)(2,1)S(1)}, bf16[1024,768]{0,1:T(8,128)(2,1)}, u32[]{:S(2)}) copy-start(bf16[1024,768]{0,1:T(8,128)(2,1)} %get-tuple-element.167) | copy-start | bytes 4718596
  478.3 77.9 %collective-permute-start.22 = (f32[224,768]{1,0:T(8,128)S(1)}, f32[224,768]{1,0:T(8,128)S(1)}, u32[]{:S(2)}, u32[]{:S(2)}) collective-permute-start(f32[224,768]{1,0:T(8,128)S(1)} %constant_dynamic-slice_fusion.6), channel_id=1, source_target_pairs={{0,2},{2,0},{4,6},{6,4},{8,10},{10,8},{12,14},{14,12},{16,18},{18,... | collective-permute-start | bytes 2064392 | tf_op jit(solution)/shard_map/ppermute | solution.py:58
  544.7 10.7 %collective-permute-start.17 = (f32[48,1152]{1,0:T(8,128)S(1)}, f32[48,1152]{1,0:T(8,128)S(1)}, u32[]{:S(2)}, u32[]{:S(2)}) collective-permute-start(f32[48,1152]{1,0:T(8,128)S(1)} %dynamic-slice_add_fusion.9), channel_id=1, source_target_pairs={{0,16},{2,18},{4,20},{6,22},{8,24},{10,26},{12,28},{14,30},{16,0},... | collective-permute-start | bytes 663560 | tf_op jit(solution)/shard_map/ppermute | solution.py:58
  548.2 10.9 %collective-permute-start.11 = (f32[88,128]{1,0:T(8,128)S(1)}, f32[88,128]{1,0:T(8,128)S(1)}, u32[]{:S(2)}, u32[]{:S(2)}) collective-permute-start(f32[88,128]{1,0:T(8,128)S(1)} %fusion.114), channel_id=1, source_target_pairs={{0,8},{2,10},{4,12},{6,14},{8,0},{10,2},{12,4},{14,6},{16,24},{18,... | collective-permute-start | bytes 135176 | tf_op jit(solution)/shard_map/ppermute | solution.py:58
  556.2 27.1 %collective-permute-start.18 = (f32[96,1152]{1,0:T(8,128)}, f32[96,1152]{1,0:T(8,128)}, u32[]{:S(2)}, u32[]{:S(2)}) collective-permute-start(f32[96,1152]{1,0:T(8,128)} %maximum_select_fusion.10), channel_id=1, source_target_pairs={{0,8},{2,10},{4,12},{6,14},{8,0},{10,2},{12,4},{14,6},{16,24},{18,... | collective-permute-start | bytes 1327112 | tf_op jit(solution)/shard_map/ppermute | solution.py:58
  557.1 28.2 %collective-permute-start.23 = (f32[112,768]{1,0:T(8,128)}, f32[112,768]{1,0:T(8,128)}, u32[]{:S(2)}, u32[]{:S(2)}) collective-permute-start(f32[112,768]{1,0:T(8,128)} %constant_dynamic-slice_fusion.5), channel_id=1, source_target_pairs={{0,8},{2,10},{4,12},{6,14},{8,0},{10,2},{12,4},{14,6},{16,24},{18,... | collective-permute-start | bytes 1032200 | tf_op jit(solution)/shard_map/ppermute | solution.py:58
  559.1 14.2 %collective-permute-start.12 = (f32[88,128]{1,0:T(8,128)S(1)}, f32[88,128]{1,0:T(8,128)S(1)}, u32[]{:S(2)}, u32[]{:S(2)}) collective-permute-start(f32[88,128]{1,0:T(8,128)S(1)} %add.340), channel_id=1, source_target_pairs={{0,16},{2,18},{4,20},{6,22},{8,24},{10,26},{12,28},{14,30},{16,0},... | collective-permute-start | bytes 135176 | tf_op jit(solution)/shard_map/ppermute | solution.py:58
  579.9 316.5 %collective-permute-start.40 = (f32[1536,768]{1,0:T(8,128)}, f32[1536,768]{1,0:T(8,128)}, u32[]{:S(2)}, u32[]{:S(2)}) collective-permute-start(f32[1536,768]{1,0:T(8,128)} %add.376), channel_id=1, source_target_pairs={{0,16},{2,18},{4,20},{6,22},{8,24},{10,26},{12,28},{14,30},{16,0},... | collective-permute-start | bytes 14155784 | tf_op jit(solution)/shard_map/ppermute | solution.py:262
  584.8 218.3 %collective-permute-start.19 = (f32[192,1152]{1,0:T(8,128)S(1)}, f32[192,1152]{1,0:T(8,128)S(1)}, u32[]{:S(2)}, u32[]{:S(2)}) collective-permute-start(f32[192,1152]{1,0:T(8,128)S(1)} %maximum_select_fusion.7), channel_id=1, source_target_pairs={{0,4},{2,6},{4,0},{6,2},{8,12},{10,14},{12,8},{14,10},{16,20},{18,... | collective-permute-start | bytes 2654216 | tf_op jit(solution)/shard_map/ppermute | solution.py:58
  586.4 205.4 %collective-permute-start.24 = (f32[56,768]{1,0:T(8,128)S(1)}, f32[56,768]{1,0:T(8,128)S(1)}, u32[]{:S(2)}, u32[]{:S(2)}) collective-permute-start(f32[56,768]{1,0:T(8,128)S(1)} %constant_dynamic-slice_fusion.4), channel_id=1, source_target_pairs={{0,16},{2,18},{4,20},{6,22},{8,24},{10,26},{12,28},{14,30},{16,0},... | collective-permute-start | bytes 516104 | tf_op jit(solution)/shard_map/ppermute | solution.py:58
  589.3 223.1 %copy-start.15 = (f32[1024,512]{1,0:T(8,128)S(1)}, f32[1024,512]{1,0:T(8,128)}, u32[]{:S(2)}) copy-start(f32[1024,512]{1,0:T(8,128)} %get-tuple-element.199) | copy-start | bytes 6291460
  589.3 273.8 %collective-permute-start.36 = (f32[384,1536]{1,0:T(8,128)S(1)}, f32[384,1536]{1,0:T(8,128)}, u32[]{:S(2)}, u32[]{:S(2)}) collective-permute-start(f32[384,1536]{1,0:T(8,128)S(1)} %maximum_select_fusion.3), channel_id=1, source_target_pairs={{0,4},{2,6},{4,0},{6,2},{8,12},{10,14},{12,8},{14,10},{16,20},{18,... | collective-permute-start | bytes 7077896 | tf_op jit(solution)/shard_map/ppermute | solution.py:58
  791.8 6.4 collective-permute-start.25
  798.2 11.9 %collective-permute-start.26 = (f32[112,768]{1,0:T(8,128)S(1)}, f32[112,768]{1,0:T(8,128)S(1)}, u32[]{:S(2)}, u32[]{:S(2)}) collective-permute-start(f32[112,768]{1,0:T(8,128)S(1)} %maximum_select_fusion.11), channel_id=1, source_target_pairs={{0,8},{2,10},{4,12},{6,14},{8,0},{10,2},{12,4},{14,6},{16,24},{18,... | collective-permute-start | bytes 1032200 | tf_op jit(solution)/shard_map/ppermute | solution.py:58
  804.4 64.0 %collective-permute-start.20 = (f32[384,1152]{1,0:T(8,128)}, f32[384,1152]{1,0:T(8,128)}, u32[]{:S(2)}, u32[]{:S(2)}) collective-permute-start(f32[384,1152]{1,0:T(8,128)} %maximum_select_fusion.4), channel_id=1, source_target_pairs={{0,2},{2,0},{4,6},{6,4},{8,10},{10,8},{12,14},{14,12},{16,18},{18,... | collective-permute-start | bytes 5308424 | tf_op jit(solution)/shard_map/ppermute | solution.py:58
  810.2 48.8 %collective-permute-start.27 = (f32[224,768]{1,0:T(8,128)S(1)}, f32[224,768]{1,0:T(8,128)S(1)}, u32[]{:S(2)}, u32[]{:S(2)}) collective-permute-start(f32[224,768]{1,0:T(8,128)S(1)} %maximum_select_fusion.8), channel_id=1, source_target_pairs={{0,2},{2,0},{4,6},{6,4},{8,10},{10,8},{12,14},{14,12},{16,18},{18,... | collective-permute-start | bytes 2064392 | tf_op jit(solution)/shard_map/ppermute | solution.py:58
  860.2 30.7 %collective-permute-start.28 = (f32[448,768]{1,0:T(8,128)}, f32[448,768]{1,0:T(8,128)}, u32[]{:S(2)}, u32[]{:S(2)}) collective-permute-start(f32[448,768]{1,0:T(8,128)} %maximum_select_fusion.5), channel_id=1, source_target_pairs={{0,4},{2,6},{4,0},{6,2},{8,12},{10,14},{12,8},{14,10},{16,20},{18,... | collective-permute-start | bytes 4128776 | tf_op jit(solution)/shard_map/ppermute | solution.py:58
  (73 other events, 550.4 us)
